TPU v7x, 128 devices: a whole 4x4x4 slice. The times are simulated.
128 devices in a mesh: node: 16 (over z, y), local: 8 (over x, core).
Axes of the slice: x: 4, y: 4, z: 4, core: 2. Of those that a mesh axis runs over, the one named last changes fastest.
Arguments:
- x: bfloat16 [128, 384, 1024], P(('node', 'local'))
- y_cot: bfloat16 [128, 384, 1024], P(('node', 'local'))
- ln1_gain: bfloat16 [2, 1024], P(None, ('node', 'local'))
- ln1_bias: bfloat16 [2, 1024], P(None, ('node', 'local'))
- qkv_weight: bfloat16 [2, 1024, 16, 192], P(None, ('node', 'local'))
- qkv_bias: bfloat16 [2, 3072], P(None, ('node', 'local'))
- out_weight: bfloat16 [2, 1024, 1024], P(None, ('node', 'local'))
- out_bias: bfloat16 [2, 1024], P(None, ('node', 'local'))
- ln2_gain: bfloat16 [2, 1024], P(None, ('node', 'local'))
- ln2_bias: bfloat16 [2, 1024], P(None, ('node', 'local'))
- up_weight: bfloat16 [2, 1024, 4096], P(None, ('node', 'local'))
- up_bias: bfloat16 [2, 4096], P(None, ('node', 'local'))
- down_weight: bfloat16 [2, 4096, 1024], P(None, ('node', 'local'))
- down_bias: bfloat16 [2, 1024], P(None, ('node', 'local'))
Outputs:
- output 1: bfloat16 [128, 384, 1024], P(('node', 'local'))
- output 2: bfloat16 [128, 384, 1024], P(('node', 'local'))
- output 3: bfloat16 [2, 1024], P(None, ('node', 'local'))
- output 4: bfloat16 [2, 1024], P(None, ('node', 'local'))
- output 5: bfloat16 [2, 1024, 16, 192], P(None, ('node', 'local'))
- output 6: bfloat16 [2, 3072], P(None, ('node', 'local'))
- output 7: bfloat16 [2, 1024, 1024], P(None, ('node', 'local'))
- output 8: bfloat16 [2, 1024], P(None, ('node', 'local'))
- output 9: bfloat16 [2, 1024], P(None, ('node', 'local'))
- output 10: bfloat16 [2, 1024], P(None, ('node', 'local'))
- output 11: bfloat16 [2, 1024, 4096], P(None, ('node', 'local'))
- output 12: bfloat16 [2, 4096], P(None, ('node', 'local'))
- output 13: bfloat16 [2, 4096, 1024], P(None, ('node', 'local'))
- output 14: bfloat16 [2, 1024], P(None, ('node', 'local'))
All inputs are finite; a program needn't handle non-finite values.
Results may differ from a plain program's by a relative error of at most 0.018346.
Values are sent between devices in bfloat16 or wider.
A program may use at most 1 GiB of HBM per device.

v0:
```python
import functools
import jax
import jax.numpy as jnp
import numpy as np
from jax import lax
from jax.experimental import pallas as pl
from jax.experimental.pallas import tpu as pltpu
from jax.sharding import PartitionSpec as P

BF16, F32 = jnp.bfloat16, jnp.float32
EPSILON = 1e-5
MESH = pl.DeviceIdType.MESH
ANY = pl.BlockSpec(memory_space=pl.ANY)
IN_VMEM = pl.BlockSpec(memory_space=pltpu.VMEM)
VMEM_LIMIT = 67 * 10**6
LAYERS, AXES, SIDE, CORES, ROWS, PARTNERS = 2, 3, 4, 2, 8, 10
CHIPS = (SIDE, SIDE, SIDE)
SHARDS = SIDE * SIDE * SIDE * CORES
SEQ, WIDTH, HIDDEN, TILE, PAIR, LN_ROWS = 384, 1024, 4096, 512, 128, 64
HEADS, HEAD, PARTS = 16, 64, 3
QKV = PARTS * WIDTH
N_TILES, N_PAIRS, N_BLOCKS = HIDDEN // TILE, WIDTH // PAIR, SEQ // PAIR
TWICE = 2 * PAIR
INV_SQRT2, INV_SQRT2PI, SCALE = 0.7071067811865476, 0.3989422804014327, 0.125
SHARES = (8, 8, 8, 8, 24, 8, 32, 8)
SIZES = tuple(SHARDS * share for share in SHARES)
OFFSETS = tuple(sum(SIZES[:k]) for k in range(len(SIZES)))
N_VEC = sum(SIZES)
GAIN1, BIAS1, GAIN2, BIAS2, QKV_BIAS, OUT_BIAS, UP_BIAS, DOWN_BIAS = range(len(SHARES))
ORDERS = ((2, 1, 0), (1, 0, 2), (0, 2, 1))
HALVES = range(2)
OWN, ONE, CROSS, TWO = range(SIDE)
ROLES = (ONE, TWO, CROSS)
A, B, C = range(AXES)
UP, DOWN, MIX = range(3)
SELF = 3


class Chip:
    def __init__(self):
        node, local = lax.axis_index('node'), lax.axis_index('local')
        self.core, self.other = lax.rem(local, CORES), 1 - lax.rem(local, CORES)
        self.where = (lax.div(node, SIDE), lax.rem(node, SIDE), lax.div(local, CORES))
        self.base = (node, local - self.core)
        self.strides = ((SIDE, 0), (1, 0), (0, CORES))
        self.near = [(v, v + 1 - 2 * parity(v), lax.rem(v + 2, SIDE), SIDE - 1 - v) for v in self.where]

        self.gaps = [near[3] - near[1] for near in self.near]

    def at(self, axis, role, half):
        near = self.near[axis]
        if role in (OWN, CROSS):
            return near[role]
        return near[role] + half * self.gaps[axis] if role == ONE else near[role] - half * self.gaps[axis]

    def device(self, axis, role, half):
        shift = self.at(axis, role, half) - self.where[axis]
        node, local = [b + shift * s if s else b for b, s in zip(self.base, self.strides[axis])]
        return (node, local + self.core)

    def partner(self):
        node, local = self.base
        return (node, local + self.other)

    def signal_partners(self, semaphore):
        for axis in range(AXES):
            for role in ROLES:
                pl.semaphore_signal(semaphore, inc=1, device_id=self.device(axis, role, A), device_id_type=MESH)
        pl.semaphore_signal(semaphore, inc=1, device_id=self.partner(), device_id_type=MESH)


def enter(chip):
    barrier = pltpu.get_barrier_semaphore()
    chip.signal_partners(barrier)
    pl.semaphore_wait(barrier, PARTNERS)


def remote(src, dst, send_sem, recv_sem, device):
    return pltpu.make_async_remote_copy(src_ref=src, dst_ref=dst, send_sem=send_sem, recv_sem=recv_sem, device_id=device,
                                        device_id_type=MESH)


def start(copies):
    for copy in copies:
        copy.start()
    return copies


def wait(copies):
    for copy in copies:
        copy.wait()


def loop(count):
    return pl.loop(0, count)


def halves(body):
    loop(len(HALVES))(body)


def parity(n):
    return lax.rem(n, 2)


def pool(sems):
    return (sems.at[n] for n in range(sems.shape[0]))


def contract(a, b, a_axis, b_axis):
    return lax.dot_general(a, b, (((a_axis,), (b_axis,)), ((), ())), preferred_element_type=F32)


def dot(a, b):
    return contract(a, b, 1, 0)


def dot_t(a, b):
    return contract(a, b, 1, 1)


def row_sum(x):
    return jnp.sum(x, axis=1, keepdims=True)


def column_sum(x):
    return jnp.sum(x, axis=0, keepdims=True)


def rounded(x):
    return x.astype(BF16).astype(F32)


def lanes(first, width=PAIR):
    return pl.ds(pl.multiple_of(first, PAIR), width)


def turn(x, cos, sin_a, sin_b):
    return x * cos + pltpu.roll(x, PAIR - ROWS, 1) * sin_a + pltpu.roll(x, ROWS, 1) * sin_b


def turn_back(d, cos, sin_a, sin_b):
    return d * cos + pltpu.roll(d * sin_a, ROWS, 1) + pltpu.roll(d * sin_b, PAIR - ROWS, 1)


def iota(shape, axis):
    return lax.broadcasted_iota(jnp.int32, shape, axis)


def block_rows(j):
    return slice(j * PAIR, (j + 1) * PAIR)


def split_heads(x):
    first = iota((PAIR, PAIR), 1) < HEAD
    rows = []
    for j in range(N_BLOCKS):
        block = x[block_rows(j)]
        rows += [jnp.where(first, block, jnp.zeros_like(block)), jnp.where(first, jnp.zeros_like(block), block)]
    return jnp.concatenate(rows, axis=0)


def total_of(chunks, join=jnp.add):
    return functools.reduce(join, chunks)


def probabilities(q_block, keys, i):
    scores = dot_t(q_block, keys)
    causal = iota((PAIR, PAIR), 0) >= iota((PAIR, PAIR), 1)
    chunks = [scores[:, block_rows(j)] * SCALE for j in range(CORES * (i + 1))]
    for head in HALVES:
        mine = slice(head, None, CORES)
        *ahead, last = chunks[mine]
        held = ahead + [jnp.where(causal, last, -1e30)]
        top = jnp.max(total_of(held, jnp.maximum), axis=1, keepdims=True)
        held = [jnp.exp(chunk - top) for chunk in held]
        inverse = 1.0 / row_sum(total_of(held))
        chunks[mine] = [chunk * inverse for chunk in held]
    return chunks


def side_by_side(chunks):
    return jnp.concatenate([chunk.astype(BF16) for chunk in chunks], axis=1)


def row_mean(x):
    return jnp.mean(x, axis=1, keepdims=True)


def normalised(h):
    center = h - row_mean(h)
    inverse = lax.rsqrt(row_mean(center * center) + EPSILON)
    return center * inverse, inverse


def half_copies(chip, src, dst, own_sem, send_sem, recv_sem):
    width = dst.shape[-1]
    mine, away = [src.at[:, lanes(which * width, width)] for which in (chip.core, chip.other)]
    place = dst.at[chip.core]
    return [pltpu.make_async_copy(mine, place, own_sem), remote(away, place, send_sem, recv_sem, chip.partner())]


class Gather:
    def __init__(self, chip, shards, fulls, sems):
        self.chip, self.shards, self.fulls = chip, shards, fulls
        self.send_sem, self.recv_sem, self.pass_send, self.pass_recv = sems

    def box(self, layer, k, half, stage, role, own=False):
        width = self.fulls[k].shape[-1] // len(HALVES)
        cols = lanes(half * width, width)
        if own:
            return self.shards[k].at[layer, :, cols]
        where = list(self.chip.where)
        for axis in ORDERS[k][:stage]:
            where[axis] = pl.ds(0, SIDE)
        axis = ORDERS[k][stage]
        where[axis] = self.chip.at(axis, role, half)
        return self.fulls[k].at[layer, where[0], where[1], where[2], self.chip.core, :, cols]

    def reach(self, layer, k, half, stage, step):
        slot, on = AXES * stage + step, stage > A and step == C
        src = self.box(layer, k, half, stage, ONE if on else OWN, stage == A)
        return remote(src, self.box(layer, k, half, stage, ONE if on else OWN), self.send_sem.at[layer, k, stage],
                      self.recv_sem.at[layer, k, half, slot], self.chip.device(ORDERS[k][stage], TWO if on else ROLES[step], half))

    def passing(self, layer, k, half, stage, step):
        role = (*ROLES, OWN)[step]
        return remote(self.box(layer, k, half, stage, role, step == SELF), self.box(layer, k, half, stage, role),
                      self.pass_send.at[layer, k], self.pass_recv.at[layer, k], self.chip.partner())

    def each(self, action):
        for k in (MIX, UP, DOWN):
            @halves
            def _(half):
                action(k, half)

    def begin(self, layer, stage):
        for step in range(C if stage else AXES):
            self.each(lambda k, half: self.reach(layer, k, half, stage, step).start())

    def own(self, layer):
        self.each(lambda k, half: self.passing(layer, k, half, A, SELF).start())

    def middle(self, layer, stage):
        def action(k, half):
            self.reach(layer, k, half, stage, A).wait_recv()
            self.reach(layer, k, half, stage, C).start()
            self.passing(layer, k, half, stage, A).start()
        self.each(action)

    def end(self, layer, stage, steps=range(AXES)):
        def action(k, half):
            for step in steps:
                self.reach(layer, k, half, stage, step).wait_recv()
                self.passing(layer, k, half, stage, step).start()
        self.each(action)

    def arrived(self, layer, k):
        box = self.fulls[k].at[layer, :, :, :, self.chip.other]
        remote(box, box, self.pass_send.at[layer, k], self.pass_recv.at[layer, k], self.chip.partner()).wait_recv()

    def left(self):
        three, full = pl.ds(0, AXES), self.fulls[UP].at[A]
        boxes = (full.at[three, A, A, A], full.at[:, three, A, A], full.at[:, :, three, A])

        @loop(LAYERS)
        def _(layer):
            @loop(AXES)
            def _(k):
                for stage, box in enumerate(boxes):
                    sem = self.send_sem.at[layer, k, stage]
                    remote(box, box, sem, sem, self.chip.partner()).wait_send()
                box, sem = full.at[:, :, :, A], self.pass_send.at[layer, k]
                remote(box, box, sem, sem, self.chip.partner()).wait_send()


def pick_lanes(sel_lane, cols):
    return (iota((PAIR, WIDTH), 0) == sel_lane[:, cols]).astype(F32).astype(BF16)


def vector_blocks():
    return [slice(k * WIDTH, (k + 1) * WIDTH) for k in range(N_VEC // WIDTH)]


def unpack_vectors(small_v, layer, sel_shard, sel_lane, vec_ref):
    tiles = small_v[...].astype(F32).reshape((SHARDS, ROWS, PAIR))
    held = jnp.sum(jnp.where(iota(tiles.shape, 1) == layer, tiles, 0.0), axis=1).astype(BF16)
    for cols in vector_blocks():
        spread = dot(held, pick_lanes(sel_lane, cols))
        spread = jnp.where(iota((SHARDS, WIDTH), 0) == sel_shard[:, cols], spread, 0.0)
        vec_ref[layer:layer + 1, cols] = column_sum(spread)


def forward_kernel(x_hbm, ycot_hbm, tables_hbm, places_hbm, up_s, down_s, mix_s, small_ref, up_f, down_f, mix_f, small_full, vec_ref,
                   dout_cols, y_hbm, h_hbm, n1_hbm, n2_hbm, ctx_hbm, act_hbm, qkv_hbm, pre_hbm, up_v, down_v, mix_v, small_v, acc, pre_v,
                   n1_v, n2_v, qkv_v, ctx_v, y_v, n1_t, n2_t, ctx_t, act_t, send_sem, recv_sem, pass_send, pass_recv,
                   small_send, small_recv, own_sems, load_sem, save_sem, share_send, share_recv, act_save, act_send, act_recv, tables,
                   places):
    shards, fulls, own_sem = (up_s, down_s, mix_s), (up_f, down_f, mix_f), pool(own_sems)
    chip = Chip()
    gather = Gather(chip, shards, fulls, (send_sem, recv_sem, pass_send, pass_recv))

    def small_copy(slot, where, device):
        place = small_full.at[(*where, chip.core)]
        return remote(place, place, small_send.at[slot], small_recv.at[slot], device)

    def small_reach(stage, step):
        where = list(chip.where)
        for axis in range(stage):
            where[axis] = pl.ds(0, SIDE)
        return small_copy(AXES * stage + step, where, chip.device(stage, ROLES[step], A))

    def small_begin(stage):
        start([small_reach(stage, step) for step in range(AXES)])

    def small_end(stage):
        for step in range(AXES):
            small_reach(stage, step).wait_recv()

    small_pass = small_copy(AXES * AXES, [pl.ds(0, SIDE)] * AXES, chip.partner())
    here = (*chip.where, chip.core)
    own = [pltpu.make_async_copy(small_ref, small_full.at[here], next(own_sem))]
    for shard, full in zip(shards, fulls):
        for layer in range(LAYERS):
            own.append(pltpu.make_async_copy(shard.at[layer], full.at[(layer, *here)], next(own_sem)))
    loads = [
        pltpu.make_async_copy(src, dst, next(own_sem)) for src, dst in ((x_hbm, y_v), (ycot_hbm, n1_v), (tables_hbm, tables), (places_hbm, places))]
    cot_copies = half_copies(chip, n1_v, dout_cols.at[LAYERS - 1], next(own_sem), next(own_sem), next(own_sem))
    start(own)
    start(loads)
    with jax.named_scope('enter'):
        enter(chip)
    with jax.named_scope('ag0'):
        gather.begin(A, A)
        gather.begin(B, A)
        wait(own)
        small_begin(A)
        gather.own(A)
        gather.own(B)
        gather.end(A, A)
    with jax.named_scope('ag1'):
        gather.begin(A, B)
        small_end(A)
        small_begin(B)
        gather.end(B, A)
        gather.begin(B, B)
        gather.middle(A, B)
        small_end(B)
        small_begin(C)
        gather.middle(B, B)
        gather.end(A, B, (B, C))
    with jax.named_scope('ag2_start'):
        gather.begin(A, C)
        small_end(C)
        small_pass.start()
        gather.end(B, B, (B, C))
    with jax.named_scope('ag2_middle'):
        gather.middle(A, C)
        gather.begin(B, C)
    with jax.named_scope('unpack'):
        small_pass.wait_recv()
        fetch = pltpu.make_async_copy(small_full, small_v, next(own_sem))
        fetch.start()
        fetch.wait()
        wait(loads)
        start(cot_copies)
        for layer in range(LAYERS):
            unpack_vectors(small_v, layer, places[A:B], places[B:C], vec_ref)
    with jax.named_scope('ag2_late'):
        gather.end(A, C, (B,))
    with jax.named_scope('ag2_end'):
        gather.end(A, C, (C,))
        wait(cot_copies)

    def saves(layer):
        pairs = [(y_v, h_hbm.at[layer]), (qkv_v, qkv_hbm.at[layer])]
        kept = [pltpu.make_async_copy(src, dst, save_sem.at[n]) for n, (src, dst) in enumerate(pairs)]
        for n, (src, dst) in enumerate(((n1_t, n1_hbm), (n2_t, n2_hbm), (ctx_t, ctx_hbm))):
            dst = dst.at[layer, chip.core]
            kept.append((pltpu.make_async_copy(src, dst, save_sem.at[CORES + n]),
                         remote(src, dst, share_send.at[layer, n], share_recv.at[layer, n], chip.partner())))
        return kept

    def quarter(layer, t):
        rows, tiles = pl.ds(t * WIDTH, WIDTH), pl.ds(CORES * t, CORES)
        src, dst = act_t.at[rows], act_hbm.at[layer, chip.core, rows]
        return [pltpu.make_async_copy(pre_v.at[tiles], pre_hbm.at[layer, tiles], act_save.at[A, t]),
                pltpu.make_async_copy(src, dst, act_save.at[B, t]),
                remote(src, dst, act_send.at[layer, t], act_recv.at[layer, t], chip.partner())]

    def settle(layer):
        _, qkv_save, *shares = saves(layer)
        qkv_save.wait()
        for share in shares:
            wait(share)

        @loop(SIDE)
        def _(t):
            wait(quarter(layer, t))

    @loop(LAYERS)
    def _(layer):
        def vector(k, first=0, width=None):
            return vec_ref[pl.ds(layer, 1), lanes(OFFSETS[k] + first, width or SIZES[k])]

        def load(k, piece):
            if k == DOWN:
                return pltpu.make_async_copy(fulls[k].at[layer, piece], down_v.at[piece], load_sem.at[k, piece])
            cols = lanes(piece * WIDTH, WIDTH)
            return pltpu.make_async_copy(fulls[k].at[layer, :, :, :, :, :, cols], (up_v, None, mix_v)[k].at[:, :, :, :, :, cols],
                                         load_sem.at[k, piece])

        def matrix(held, piece):
            return held[:, :, :, :, :, lanes(piece * WIDTH, WIDTH)].reshape((WIDTH, WIDTH))

        def have(k):
            gather.arrived(layer, k)

        def meanwhile(action):
            @pl.when(layer == A)
            def _():
                action()

        h_save, qkv_save, n1_share, n2_share, ctx_share = saves(layer)
        with jax.named_scope('have_mix'):
            have(MIX)
            start([load(MIX, k) for k in range(SIDE)])

        h_save.start()

        @pl.when(layer == B)
        def _():
            settle(A)

        with jax.named_scope('ln'):
            @loop(SEQ // LN_ROWS)
            def _(r):
                rows = pl.ds(pl.multiple_of(r * LN_ROWS, LN_ROWS), LN_ROWS)
                scaled, _ = normalised(y_v[rows, :].astype(F32))
                n1_v[rows, :] = (scaled * vector(GAIN1) + vector(BIAS1)).astype(BF16)
                n2_v[rows, :] = (scaled * vector(GAIN2) + vector(BIAS2)).astype(BF16)

        for src, dst, share in ((n1_v, n1_t, n1_share), (n2_v, n2_t, n2_share)):
            dst[...] = src[...].T
            start(share)

        with jax.named_scope('qkv'):
            for k in range(PARTS):
                load(MIX, k).wait()
                x = dot(n1_v[...], matrix(mix_v, k)) + vector(QKV_BIAS, k * WIDTH, WIDTH)
                for c in range(N_PAIRS):
                    block = x[:, block_rows(c)]
                    if k < C:
                        block = turn(block, *[tables[n] for n in range(PARTS)])
                    qkv_v[:, lanes(k * WIDTH + c * PAIR)] = block.astype(BF16)

        qkv_save.start()
        with jax.named_scope('have_up'):
            have(UP)
            have(DOWN)

        start([load(UP, k) for k in range(SIDE)] + [load(DOWN, k) for k in range(SIDE)])
        with jax.named_scope('fattn'):
            def one_pair(pair):
                keys = split_heads(qkv_v[:, lanes(WIDTH + pair * PAIR)])
                values = split_heads(qkv_v[:, lanes(C * WIDTH + pair * PAIR)])
                for i in range(N_BLOCKS):
                    n = (i + 1) * CORES * PAIR
                    probs = probabilities(qkv_v[block_rows(i), lanes(pair * PAIR)], keys[:n], i)
                    ctx_v[block_rows(i), lanes(pair * PAIR)] = dot(side_by_side(probs), values[:n]).astype(BF16)

            @loop(N_PAIRS // CORES)
            def _(two):
                for k in HALVES:
                    one_pair(CORES * two + k)

                @pl.when((layer == A) & (two == A))
                def _():
                    gather.middle(B, C)

        ctx_t[...] = ctx_v[...].T
        start(ctx_share)
        with jax.named_scope('fout'):
            load(MIX, PARTS).wait()
            acc[...] = y_v[...].astype(F32) + dot(ctx_v[...], matrix(mix_v, PARTS)) + (vector(OUT_BIAS) + vector(DOWN_BIAS))

        with jax.named_scope('fmlp'):
            @loop(SIDE)
            def _(t):
                cols = lanes(t * WIDTH, WIDTH)
                load(UP, t).wait()
                pre = dot(n2_v[...], matrix(up_v, t)) + vector(UP_BIAS, t * WIDTH, WIDTH)
                for k in HALVES:
                    pre_v[CORES * t + k] = pre[:, k * TILE:(k + 1) * TILE]
                act = (0.5 * pre * (1.0 + lax.erf(pre * INV_SQRT2))).astype(BF16)
                act_t[cols, :] = act.T
                start(quarter(layer, t))
                load(DOWN, t).wait()
                acc[...] += dot(act, down_v[t].reshape((WIDTH, WIDTH)))

                @pl.when((layer == A) & (t == B))
                def _():
                    gather.end(B, C, (B,))

        h_save.wait()
        y_v[...] = acc[...].astype(BF16)
        with jax.named_scope('fend'):
            meanwhile(lambda: gather.end(B, C, (C,)))

    with jax.named_scope('ftail'):
        last = pltpu.make_async_copy(y_v, y_hbm, next(own_sem))
        last.start()
        for stage in range(AXES):
            for step in range(AXES):
                small_reach(stage, step).wait_send()
        small_pass.wait_send()
        gather.left()
        settle(LAYERS - 1)
        last.wait()


def forward(x, y_cot, shards, small_tile, tables, places):
    grid = CHIPS + (CORES,)
    full = [(LAYERS,) + grid + tensor.shape[1:] for tensor in shards]
    shapes = [(shape, BF16) for shape in full] + [(grid + small_tile.shape, BF16), ((LAYERS, N_VEC), F32), ((LAYERS, CORES, SEQ, TILE), BF16), ((SEQ, WIDTH), BF16),
                                                  ((LAYERS, SEQ, WIDTH), BF16)]
    shapes += [((LAYERS, CORES, width, SEQ), BF16) for width in (WIDTH, WIDTH, WIDTH, HIDDEN)]
    shapes += [((LAYERS, SEQ, QKV), BF16), ((LAYERS, N_TILES, SEQ, TILE), F32)]
    dma = pltpu.SemaphoreType.DMA
    slots = AXES * AXES
    scratch = [pltpu.VMEM(shape[1:], BF16) for shape in full] + [pltpu.VMEM(grid + small_tile.shape, BF16)]
    scratch += [pltpu.VMEM((SEQ, WIDTH), F32), pltpu.VMEM((N_TILES, SEQ, TILE), F32)]
    scratch += [pltpu.VMEM((SEQ, width), BF16) for width in (WIDTH, WIDTH, QKV, WIDTH, WIDTH)]
    scratch += [pltpu.VMEM((width, SEQ), BF16) for width in (WIDTH, WIDTH, WIDTH, HIDDEN)]
    scratch += [dma(shape) for shape in ((LAYERS, AXES, AXES), (LAYERS, AXES, len(HALVES), slots), (LAYERS, AXES), (LAYERS, AXES))]
    scratch += [dma(shape) for shape in ((slots + 1,), (slots + 1,), (slots + SIDE + SIDE + AXES,), (AXES, SIDE), (SIDE + 1,), (LAYERS, AXES), (LAYERS, AXES), (CORES, SIDE), (LAYERS, SIDE), (LAYERS, SIDE))]
    scratch += [pltpu.VMEM(tables.shape, F32), pltpu.VMEM(places.shape, jnp.int32)]
    out_specs = [IN_VMEM if dtype == F32 and len(shape) == LAYERS else ANY for shape, dtype in shapes]
    return pl.pallas_call(
        forward_kernel,
        out_shape=[jax.ShapeDtypeStruct(*s) for s in shapes],
        in_specs=[ANY] * SIDE + [IN_VMEM] * SIDE,
        out_specs=out_specs,
        scratch_shapes=scratch,
        compiler_params=pltpu.CompilerParams(collective_id=0, has_side_effects=True, vmem_limit_bytes=VMEM_LIMIT),
        name='forward_layers',
    )(x, y_cot, tables, places, *shards, small_tile)


WAVES = ((384, 384, 512), (384, 384, 256), (256, 256, 256))
LEADS = ((2,) + CHIPS[1:], CHIPS[1:], (2, SIDE), (SIDE,), (AXES,))
W_UP, W_DOWN, W_QKV, W_OUT = range(4)
STEPS = ((1, (2,)), (0, ()), (2, (4, 3)), (4, (5,)), (3, ()), (5, (6, 7, 8)), (8, (9,)), (9, ()))
LAST = AXES * AXES
CARRIED = ((0, 6, 0), (1, 4, 0), (2, 0, 0))
US_COLUMN, US_HOP, US_ADD, US_STEP = 0.022, 2.5, 0.0013, 0.2
US_FIRST, US_OUT, US_TILE, US_GRADIENT, US_PAIR, US_NORM = 2, 1.4, 1.6, 0.0035, 3.6, 2.7


class Schedule:
    def __init__(self):
        self.now, self.free, self.lines = 0.0, {}, []

    def send(self, link, columns):
        self.free[link] = max(self.free.get(link, 0.0), self.now) + columns * US_COLUMN
        return self.free[link] + US_HOP

    def due(self, limit):
        found = []
        while self.lines:
            line = min(self.lines, key=lambda one: one[A][A]())
            ready = line[A][A]()
            if limit is not None and ready > limit:
                break
            _, run, sends, cost = line.pop(A)
            self.lines = [one for one in self.lines if one]
            self.now = max(self.now, ready) + cost
            sends()
            found.append(run)
        return found

    def finish(self, line):
        while line:
            ready, run, sends, cost = line.pop(A)
            self.now = max(self.now, ready()) + cost
            sends()
            run()
        self.lines = [one for one in self.lines if one]

    def run(self, limit):
        for step in self.due(limit):
            step()

    def passed(self, cost):
        self.now += cost
        self.run(self.now)

    def hooks(self, count, cost):
        planned = []
        for _ in range(count):
            self.now += cost
            planned.append(self.due(self.now))
        return planned


def at_hooks(n, planned):
    for when, steps in enumerate(planned):
        if steps:
            @pl.when(n == when)
            def _():
                for step in steps:
                    step()


def add_into(dst, src, n_axes):
    if n_axes < 2:
        dst[...] += src[...]
        return

    @loop(SIDE)
    def _(k):
        dst[k] += src[k]


def at_axis(ref, axis, value, n_axes):
    every = [pl.ds(0, SIDE)] * n_axes
    every[axis] = value
    return ref.at[tuple(every)]


class Reduce:
    def __init__(self, chip, schedule, wave, grads, came, fin, sems, spare, write, done, when=None):
        self.wave, self.chip, self.schedule, self.widths, self.grads = wave, chip, schedule, WAVES[wave], grads
        self.came, self.fin, (self.send_sem, self.recv_sem), (self.spare, self.spare_sem) = came, fin, sems, spare
        self.write, self.done, self.when, self.times = write, done, when, {}

    def box(self, a, half, stage):
        order = ORDERS[a]
        ref = self.came[a][A].at[half, A]
        spot = [axis for axis in range(AXES) if axis != order[A]].index(order[B])
        if stage == B:
            return ref, spot, C
        return at_axis(ref, spot, self.chip.where[order[B]], C), A, B

    def copy(self, a, half, slot):
        stage, turn = divmod(slot, AXES)
        sems = self.send_sem.at[a, stage], self.recv_sem.at[a, half, slot]
        if slot == LAST:
            return remote(self.total(a, half).at[self.chip.other], self.fin[a].at[half], *sems, self.chip.partner())
        axis = ORDERS[a][stage]
        if stage == C:
            role = value = ROLES[turn]
            dst = self.came[a][SIDE].at[half, turn]
        else:
            role, value = TWO if turn == C else ONE, (ONE, CROSS, TWO)[turn]
            dst = self.came[a][CORES * stage + turn // C].at[half]
            dst = dst if turn == C else dst.at[turn]
        value = self.chip.at(axis, value, half)
        if stage:
            ref, spot, n_axes = self.box(a, half, stage)
            src = at_axis(ref, spot, value, n_axes)
        else:
            src = self.came[a][A].at[half, B] if turn == C else at_axis(self.grads[a].at[half], axis, value, AXES)
        return remote(src, dst, *sems, self.chip.device(axis, role, half))

    def each(self, action):
        for a in range(AXES):
            halves(lambda half: action(a, half))

    def sending(self, slot):
        stage = slot // AXES
        share = SIDE ** (CORES * stage)
        self.times[slot] = self.schedule.now + US_HOP if slot == LAST else max(
            self.schedule.send(ORDERS[a][stage], self.widths[a] / share) for a in range(AXES))

    def begin(self):
        for slot in (B, A):
            self.each(lambda a, half: self.copy(a, half, slot).start())

    def plan(self, first=0, last=None, late=0):
        for slot in (B, A):
            self.times[slot] = self.schedule.now + late
            if not first:
                self.sending(slot)
        for _, sent in STEPS[:first]:
            self.times.update((slot, self.schedule.now + late + US_HOP) for slot in sent)
        line = [
            (lambda slot=slot: self.times[slot], lambda k=k: self.step(k), lambda sent=sent: [self.sending(n) for n in sent],
             CORES * US_ADD * sum(self.widths) if k < C else US_STEP) for k, (slot, sent) in enumerate(STEPS)][first:last]
        self.schedule.lines.append(line)
        return line

    def step(self, k):
        def work():
            with jax.named_scope(f'w{self.wave}s{k}'):
                (self.first, self.first, self.halve, self.settle, self.settle, self.spread, self.cross, self.finish)[k](STEPS[k][A])
        if self.when is None:
            work()
        else:
            pl.when(self.when)(work)

    def held(self, a, half):
        ref = self.spare[A].at[a] if a < C else self.spare[B]
        return ref.at[half, :, :, :, :, pl.ds(0, self.widths[a])]

    def first(self, slot):
        def local(a, half):
            axis = ORDERS[a][A]
            return pltpu.make_async_copy(at_axis(self.grads[a].at[half], axis, self.chip.at(axis, TWO if slot else OWN, half), AXES),
                                         self.held(a, half), self.spare_sem.at[a, half])

        def action(a, half):
            local(a, half).wait()
            self.copy(a, half, slot).wait_recv()
            add_into(self.came[a][A].at[half, slot], self.held(a, half), C)
            if slot:
                self.copy(a, half, C).start()

        self.each(lambda a, half: local(a, half).start())
        self.each(action)

    def halve(self, slot):
        def action(a, half):
            ref, spot, n_axes = self.box(a, half, B)
            self.copy(a, half, slot).wait_recv()
            for turn, role in ((B, CROSS), (A, ONE), (C, TWO), (C, OWN)):
                value = self.chip.at(ORDERS[a][B], role, half)
                add_into(at_axis(ref, spot, value, n_axes), at_axis(self.came[a][B].at[half], spot, value, n_axes), B)
                if turn < C:
                    self.copy(a, half, AXES + turn).start()
        self.each(action)

    def settle(self, slot):
        def action(a, half):
            ref, spot, n_axes = self.box(a, half, B)
            self.copy(a, half, slot).wait_recv()
            value = self.chip.at(ORDERS[a][B], TWO if slot > AXES else OWN, half)
            add_into(at_axis(ref, spot, value, n_axes), self.came[a][C].at[half, slot - AXES], B)
            if slot > AXES:
                self.copy(a, half, AXES + C).start()
        self.each(action)

    def spread(self, slot):
        def action(a, half):
            ref, *_ = self.box(a, half, C)
            self.copy(a, half, slot).wait_recv()
            add_into(ref, self.came[a][AXES].at[half], B)
            for turn in range(AXES):
                self.copy(a, half, CORES * AXES + turn).start()
        self.each(action)

    def total(self, a, half):
        ref, *_ = self.box(a, half, C)
        return ref.at[self.chip.where[ORDERS[a][C]]]

    def cross(self, _):
        def action(a, half):
            for turn in range(AXES):
                self.copy(a, half, CORES * AXES + turn).wait_recv()
            self.total(a, half)[...] += total_of([self.came[a][SIDE][half, turn] for turn in range(AXES)])
            self.copy(a, half, LAST).start()
        self.each(action)

    def finish(self, _):
        def action(a, half):
            self.write(a, half, self.chip.core, self.total(a, half)[self.chip.core])
            self.copy(a, half, LAST).wait_recv()
            self.write(a, half, self.chip.other, self.fin[a][half])
        self.each(action)
        three = pl.ds(0, AXES)
        for a, (grad, fin) in enumerate(zip(self.grads, self.fin)):
            for stage, block in enumerate((grad.at[:, :, :, three], grad.at[:, :, three, A], grad.at[:, three, A, A], fin)):
                sem = self.send_sem.at[a, stage]
                remote(block, block, sem, sem, self.chip.partner()).wait_send()
        self.done()


class VectorSum:
    def __init__(self, chip, schedule, total, came, sems, finish, when=None):
        self.schedule, self.total, self.came, self.sems, self.finish, self.when, self.ready = schedule, total, came, sems, finish, when, 0.0
        self.devices = [[chip.device(axis, role, A) for role in ROLES] for axis in range(AXES)] + [[chip.partner()]]

    def copies(self, k):
        return [remote(self.total, self.came.at[AXES * k + n], self.sems.at[A, AXES * k + n], self.sems.at[B, AXES * k + n], device)
                for n, device in enumerate(self.devices[k])]

    def sending(self, k):
        if k < SIDE:
            self.ready = self.schedule.send(k, N_VEC / (SIDE * SIDE * ROWS))

    def step(self, k):
        def work():
            with jax.named_scope(f'vec{k}'):
                wait(self.copies(k - 1))
                for n in range(len(self.devices[k - 1])):
                    self.total[...] += self.came[AXES * (k - 1) + n]
            if k < SIDE:
                start(self.copies(k))
            else:
                self.finish()
        if self.when is None:
            work()
        else:
            pl.when(self.when)(work)

    def begin(self):
        start(self.copies(A))

    def plan(self):
        self.sending(A)
        self.schedule.lines.append([
            (lambda: self.ready, lambda k=k: self.step(k), lambda k=k: self.sending(k), US_STEP) for k in range(1, SIDE + 1)])


def backward_kernel(ycot_hbm, tables, vec_ref, places, up_hbm, down_hbm, mix_hbm, h_hbm, n1_hbm, n2_hbm, ctx_hbm,
                    act_hbm, qkv_hbm, pre_hbm, _, dx_hbm, small_ref, up_sum, down_sum, qkv_sum, out_sum, dout_cols, dpre_cols,
                    dqkv_cols, *refs):
    n_arrays, sums = AXES * len(WAVES), (up_sum, down_sum, qkv_sum, out_sum)
    grads, refs = refs[:n_arrays], refs[n_arrays:]
    (spare, spare_wide, tile_v, big_v, rhs_v, wup_v, wdown_v, pre_v, dn1, dn2, dctx, dk_acc, dv_acc, qkv_v, dpre_v, dqkv_v, dh_v, h_v,
     totals, came_vec, send_sem, recv_sem, spare_sem, tile_sem, big_sem, rhs_sem, mlp_sem, io_sem, own_sem, share_send,
     share_recv, pre_sem, vec_sem, credit, *refs) = refs
    fins, came = refs[:n_arrays], refs[n_arrays:]
    first_in = pltpu.make_async_copy(ycot_hbm, dh_v, io_sem.at[A])
    first_in.start()
    chip = Chip()
    core, other = chip.core, chip.other

    def exchange(layer, k, src, dst):
        return half_copies(chip, src, dst.at[layer], own_sem.at[k], share_send.at[k], share_recv.at[k])

    def tokens_load(layer, src, part, slot):
        return [pltpu.make_async_copy(src.at[layer, k, pl.ds(part * WIDTH, WIDTH)], big_v.at[slot, :, pl.ds(k * SEQ, SEQ)],
                                      big_sem.at[slot, k]) for k in range(CORES)]

    def weight_load(layer, k, slot):
        return pltpu.make_async_copy(mix_hbm.at[layer, :, lanes(k * WIDTH, WIDTH)], big_v.at[slot], big_sem.at[slot, CORES])

    def tile_loads(layer, t, slot):
        rows = lanes(t * TILE, TILE)
        pairs = ((down_hbm.at[layer, rows], wdown_v), (pre_hbm.at[layer, t], pre_v), (up_hbm.at[layer, :, rows], wup_v))
        return [pltpu.make_async_copy(src, dst.at[slot], mlp_sem.at[slot, n]) for n, (src, dst) in enumerate(pairs)]

    def input_loads(layer):
        return [pltpu.make_async_copy(qkv_hbm.at[layer], qkv_v, io_sem.at[B]), pltpu.make_async_copy(h_hbm.at[layer], h_v, io_sem.at[C])]

    def rhs_load(layer, src, first, width, k):
        cols = lanes(first, width)
        return [pltpu.make_async_copy(src.at[layer, n, :, cols], rhs_v.at[pl.ds(n * SEQ, SEQ), cols], rhs_sem.at[k, n])
                for n in range(CORES)]

    def prefetch(layer):
        start(tokens_load(layer, ctx_hbm, A, AXES) + tokens_load(layer, act_hbm, A, A))

    def prefetch_more(layer):
        start(tokens_load(layer, act_hbm, B, B) + tokens_load(layer, act_hbm, C, C) + input_loads(layer))
        for t in HALVES:
            start(tile_loads(layer, t, t))

    prefetch(LAYERS - 1)
    start(rhs_load(LAYERS - 1, dout_cols, A, TILE, A))
    prefetch_more(LAYERS - 1)
    with jax.named_scope('enter'):
        enter(chip)
    with jax.named_scope('first_in'):
        first_in.wait()
    dx_copy = pltpu.make_async_copy(dh_v, dx_hbm, io_sem.at[A])

    def vector_at(k, first=0, width=None):
        return lanes(OFFSETS[k] + first, width or SIZES[k])

    def reduction(schedule, layer, wave, when):
        def write(a, half, side, block):
            def put(arr, group, col, first, width):
                size = sums[arr].shape[-1] // CORES
                sums[arr][layer, group, :, lanes(side * size + col, width)] = block[:, first:first + width].astype(BF16)
            width, colour = WAVES[wave][a], CORES * a + half
            if wave:
                first = colour * width if wave == C or a < C else SIDE * WAVES[wave][A] + half * width
                put(W_QKV if wave == C else W_UP, A, first, A, width)
            elif a < C:
                put(W_DOWN, colour, A, A, width)
            else:
                for k in HALVES:
                    put(W_DOWN, CORES * half + k, WAVES[A][A], k * PAIR, PAIR)
                put(W_OUT, A, half * TWICE, TWICE, TWICE)

        def done():
            @pl.when(layer == LAYERS - 1)
            def _():
                chip.signal_partners(credit.at[wave])

        where = slice(AXES * wave, AXES * (wave + 1))
        count = len(LEADS)
        return Reduce(chip, schedule, wave, [grad.at[layer] for grad in grads[where]],
                      [came[count * (AXES * wave + a):count * (AXES * wave + a + 1)] for a in range(AXES)],
                      fins[where], (send_sem.at[wave], recv_sem.at[wave]), ((spare, spare_wide), spare_sem), write, done, when)

    def vector_sum(schedule, layer, when):
        def own_part():
            with jax.named_scope('own'):
                node, local = chip.base
                me = node * (SIDE * CORES) + local + core
                row = jnp.zeros((ROWS, PAIR), F32)
                for k, share in enumerate(SHARES):
                    if k == QKV_BIAS:
                        firsts = [part * WIDTH + lax.div(me, CORES * ROWS) * PAIR for part in range(PARTS)]
                    else:
                        firsts = [lax.div(me * share, PAIR) * PAIR]
                    for first in firsts:
                        cols = lanes(OFFSETS[k] + first)
                        left = jnp.zeros((ROWS, PAIR), F32) + totals[layer, :, cols] * (places[A:B, cols] == me).astype(F32)
                        pick = (iota((PAIR, PAIR), 0) == places[B:C, cols]).astype(F32).astype(BF16)
                        for _ in range(PARTS):
                            row = row + dot_t(left.astype(BF16), pick)
                            left = left - rounded(left)
                small_ref[layer] = row.astype(BF16)

            @pl.when(layer == LAYERS - 1)
            def _():
                chip.signal_partners(credit.at[AXES])

        return VectorSum(chip, schedule, totals.at[layer], came_vec, vec_sem, own_part, when)

    def run_on(schedule, layer, when):
        lines = [reduction(schedule, layer, wave, when).plan(step, late=late) for wave, step, late in CARRIED]
        vector_sum(schedule, layer, when).plan()
        return lines

    @loop(LAYERS + 1)
    def _(turn_no):
        layer = LAYERS - 1 - turn_no
        working = pl.when(turn_no < LAYERS)
        total = totals.at[layer]
        schedule = Schedule()

        carried = run_on(schedule, layer + 1, turn_no > A)

        def product(lhs_slot, first, width, out_slot):
            value = dot(big_v[lhs_slot, :, 0:CORES * SEQ], rhs_v[:, lanes(first, width)])
            tile_v[out_slot, :, :, :, :, :, 0:width] = value.reshape(CHIPS + (CORES, ROWS, width))

        def tile_out(slot, src, dst):
            return pltpu.make_async_copy(src, dst, tile_sem.at[slot])

        def tile_done(slot, width):
            block = tile_v.at[slot, :, :, :, :, :, pl.ds(0, width)]
            tile_out(slot, block, block).wait()

        def columns(wave, a, half, first, width):
            return grads[AXES * wave + a].at[layer, half, :, :, :, :, :, pl.ds(first, width)]

        def launch(wave):
            schedule.finish(carried[wave])

            @pl.when(turn_no == B)
            def _():
                pl.semaphore_wait(credit.at[wave], PARTNERS)

            current = reduction(schedule, layer, wave, turn_no < LAYERS)
            if wave == C:
                @pl.when(turn_no == B)
                def _():
                    pl.semaphore_wait(credit.at[AXES], PARTNERS)

                @working
                def _():
                    vector_sum(schedule, layer, None).begin()

            working(current.begin)
            if wave < C:
                current.plan(last=CARRIED[wave][B])

        @working
        def _():
            with jax.named_scope('dw_out'):
                @pl.when(turn_no == B)
                def _():
                    wait(exchange(layer, A, dh_v, dout_cols))
                    start(rhs_load(layer, dout_cols, A, TILE, A))

                wait(rhs_load(layer, dout_cols, A, TILE, A))
                wait(tokens_load(layer, ctx_hbm, A, AXES))
                product(AXES, A, TILE, B)
                start(tokens_load(layer, act_hbm, AXES, AXES))
                for k in HALVES:
                    tile_out(B, tile_v.at[B, :, :, :, :, :, pl.ds(k * TWICE, TWICE)], columns(A, C, k, TWICE, TWICE)).start()

        schedule.passed(US_FIRST)
        out_hooks = schedule.hooks(SIDE, US_OUT)

        @loop(SIDE)
        def _(z):
            @working
            def _():
                slot = parity(z)
                wait(tokens_load(layer, act_hbm, z, z))

                @pl.when(z > A)
                def _():
                    tile_done(slot, TILE)

                product(z, A, TILE, slot)
                split = WAVES[A][A]
                for k in range(SIDE):
                    a, half = divmod(k, CORES)
                    for c in range(CORES):
                        block = tile_v.at[slot, :, :, CORES * c + a, half]
                        tile_out(slot, block.at[:, :, :, pl.ds(0, split)], grads[a].at[layer, half, z, :, :, c]).start()
                        tile_out(slot, block.at[:, :, :, pl.ds(split, PAIR)],
                                 grads[C].at[layer, a, z, :, :, c, :, pl.ds(half * PAIR, PAIR)]).start()

            at_hooks(z, out_hooks)

        @working
        def _():
            start(tokens_load(layer, n2_hbm, A, A) + [weight_load(layer, k, k + 1) for k in range(PARTS)])
            for slot in HALVES:
                tile_done(slot, TILE)

        schedule.passed(US_STEP)
        launch(A)

        @working
        def _():
            dn2[...] = jnp.zeros_like(dn2)

        def pre_copy(t, slot, away):
            place = dpre_cols.at[layer, core, :, lanes(lax.rem(t, SIDE) * TILE, TILE)]
            if away:
                return remote(dpre_v.at[slot], place, pre_sem.at[A, t], pre_sem.at[B, t], chip.partner())
            return pltpu.make_async_copy(dpre_v.at[slot], place, own_sem.at[CORES + slot])

        def pre_act(t, leave):
            for away, whose in ((False, core), (True, other)):
                @pl.when(lax.div(t, SIDE) == whose)
                def _():
                    copy = pre_copy(t, parity(t), away)
                    if leave:
                        copy.start()
                    elif away:
                        copy.wait_send()
                    else:
                        copy.wait()

        tile_hooks = schedule.hooks(N_TILES, US_TILE)

        with jax.named_scope('mlp'):
            @loop(N_TILES)
            def _(t):
                @working
                def _():
                    slot = parity(t)
                    wait(tile_loads(layer, t, slot))
                    d_act = rounded(dot_t(dh_v[...], wdown_v[slot]))
                    pre = pre_v[slot]
                    slope = 0.5 * (1.0 + lax.erf(pre * INV_SQRT2)) + pre * (INV_SQRT2PI * jnp.exp(-0.5 * pre * pre))
                    d_pre = d_act * slope
                    total[:, vector_at(UP_BIAS, t * TILE, TILE)] = column_sum(d_pre)

                    @pl.when(t > B)
                    def _():
                        pre_act(t - CORES, False)

                    dpre_v[slot] = d_pre.astype(BF16)
                    pre_act(t, True)
                    dn2[...] += dot_t(dpre_v[slot], wup_v[slot])

                    @pl.when(t + CORES < N_TILES)
                    def _():
                        start(tile_loads(layer, t + CORES, slot))

                at_hooks(t, tile_hooks)

        @working
        def _():
            for t in HALVES:
                pre_act(N_TILES - CORES + t, False)
            for t in range(SIDE):
                pre_copy(SIDE * core + t, A, True).wait_recv()

        def gradient_loads(wave, source):
            first = 0
            for a in range(AXES):
                width = CORES * WAVES[wave][a]
                start(rhs_load(layer, source, first, width, a))
                first += width

        def gradient_wave(wave, source, lhs_slot, first, orders):
            split, count = WAVES[wave][orders[A]], len(orders)
            width = CORES * split
            planned = schedule.hooks(count, width * US_GRADIENT)

            @loop(count)
            def _(n):
                @working
                def _():
                    slot = parity(n)
                    wait(rhs_load(layer, source, first + n * width, width, orders[A] + n))

                    @pl.when(n > B)
                    def _():
                        tile_done(slot, width)

                    product(lhs_slot, first + n * width, width, slot)
                    for k, a in enumerate(orders):
                        @pl.when(n == k)
                        def _():
                            for half in HALVES:
                                block = tile_v.at[slot, :, :, :, :, :, pl.ds(half * split, split)]
                                tile_out(slot, block, columns(wave, a, half, 0, split)).start()

                at_hooks(n, planned)

            @working
            def _():
                for slot in range(min(count, CORES)):
                    tile_done(slot, width)

        @working
        def _():
            gradient_loads(B, dpre_cols)
            wait(tokens_load(layer, n2_hbm, A, A))

        with jax.named_scope('dw1'):
            gradient_wave(B, dpre_cols, A, A, (A, B))
            gradient_wave(B, dpre_cols, A, SIDE * WAVES[B][A], (C,))
        launch(B)
        @working
        def _():
            weight_load(layer, AXES, A).start()
            d_sum = column_sum(dh_v[...].astype(F32))
            total[:, vector_at(OUT_BIAS)] = d_sum
            total[:, vector_at(DOWN_BIAS)] = d_sum
            wait(input_loads(layer))
            weight_load(layer, AXES, A).wait()
            dctx[...] = dot_t(dh_v[...], big_v[A]).astype(BF16)

        pair_hooks = schedule.hooks(N_PAIRS // CORES, US_PAIR)

        with jax.named_scope('attn'):
            def one_pair(pair, dk_sum, dv_sum):
                at = lanes(pair * PAIR)
                keys = split_heads(qkv_v[:, lanes(WIDTH + pair * PAIR)])
                values = split_heads(qkv_v[:, lanes(C * WIDTH + pair * PAIR)])
                q_t = qkv_v[:, at].T
                dc_t = dctx[:, at].T
                bias_sums = [jnp.zeros((1, PAIR), F32)] * PARTS

                def turned_back(n, d, rows, to):
                    d = turn_back(rounded(d), *[tables[k, rows, :] for k in range(PARTS)])
                    bias_sums[n] = bias_sums[n] + column_sum(d)
                    dqkv_v[rows, to] = d.astype(BF16)

                for i in range(N_BLOCKS):
                    old, n = i * TWICE, (i + 1) * TWICE
                    rows = block_rows(i)
                    probs = probabilities(qkv_v[rows, at], keys[:n], i)
                    d_all = rounded(dot_t(dctx[rows, at], values[:n]))
                    d_scores = [d_all[:, block_rows(j)] for j in range(CORES * (i + 1))]
                    for head in HALVES:
                        mine = slice(head, None, CORES)
                        mean = row_sum(total_of([p * d for p, d in zip(probs[mine], d_scores[mine])]))
                        d_scores[mine] = [p * (d - mean) * SCALE for p, d in zip(probs[mine], d_scores[mine])]
                    d_scores, probs = side_by_side(d_scores), side_by_side(probs)
                    turned_back(A, dot(d_scores, keys[:n]), rows, at)
                    for acc, left, right in ((dk_sum, q_t, d_scores), (dv_sum, dc_t, probs)):
                        part = dot(left[:, rows], right)
                        if i:
                            acc[:, :old] += part[:, :old]
                        acc[:, old:n] = part[:, old:]
                first = iota((PAIR, PAIR), 0) < HEAD
                for j in range(N_BLOCKS):
                    rows = block_rows(j)
                    d_key, d_value = [jnp.where(first, acc[:, block_rows(CORES * j)], acc[:, block_rows(CORES * j + 1)]).T
                                      for acc in (dk_sum, dv_sum)]
                    turned_back(B, d_key, rows, lanes(WIDTH + pair * PAIR))
                    d_value = d_value.astype(BF16)
                    bias_sums[C] = bias_sums[C] + column_sum(d_value.astype(F32))
                    dqkv_v[rows, lanes(C * WIDTH + pair * PAIR)] = d_value
                for k, bias_sum in enumerate(bias_sums):
                    total[:, vector_at(QKV_BIAS, k * WIDTH + pair * PAIR, PAIR)] = bias_sum

            @loop(N_PAIRS // CORES)
            def _(two):
                @working
                def _():
                    for k in HALVES:
                        one_pair(CORES * two + k, dk_acc.at[k], dv_acc.at[k])

                at_hooks(two, pair_hooks)

        @working
        def _():
            start(exchange(layer, B, dqkv_v, dqkv_cols))
            dn1[...] = jnp.zeros_like(dn1)

            with jax.named_scope('dn1'):
                @loop(PARTS)
                def _(k):
                    weight_load(layer, k, k + 1).wait()
                    dn1[...] += dot_t(dqkv_v[:, lanes(k * WIDTH, WIDTH)], big_v[k + 1])

            start(tokens_load(layer, n1_hbm, A, B))

        schedule.passed(US_NORM)

        @working
        def _():
            for k in (GAIN1, BIAS1, GAIN2, BIAS2):
                total[:, vector_at(k)] = jnp.zeros((1, WIDTH), F32)

            with jax.named_scope('lnb'):
                @loop(SEQ // LN_ROWS)
                def _(r):
                    rows = pl.ds(pl.multiple_of(r * LN_ROWS, LN_ROWS), LN_ROWS)
                    scaled, inverse = normalised(h_v[rows, :].astype(F32))
                    d1, d2 = rounded(dn1[rows, :]), rounded(dn2[rows, :])
                    for k, value in ((GAIN1, d1 * scaled), (BIAS1, d1), (GAIN2, d2 * scaled), (BIAS2, d2)):
                        total[:, vector_at(k)] += column_sum(value)
                    g1, g2 = [vec_ref[pl.ds(layer, 1), lanes(OFFSETS[k], WIDTH)] for k in (GAIN1, GAIN2)]
                    d_scaled = d1 * g1 + d2 * g2
                    d_h = inverse * (d_scaled - row_mean(d_scaled) - scaled * row_mean(d_scaled * scaled))
                    dh_v[rows, :] = (dh_v[rows, :].astype(F32) + d_h).astype(BF16)

        schedule.passed(US_NORM)
        @working
        def _():
            wait(exchange(layer, B, dqkv_v, dqkv_cols))
            gradient_loads(C, dqkv_cols)
            wait(tokens_load(layer, n1_hbm, A, B))

        @pl.when(turn_no == A)
        def _():
            start(exchange(layer - 1, A, dh_v, dout_cols))

        @pl.when(turn_no == B)
        def _():
            dx_copy.start()

        with jax.named_scope('dw2'):
            gradient_wave(C, dqkv_cols, B, A, (A, B, C))

        @pl.when(turn_no == A)
        def _():
            prefetch(layer - 1)
            prefetch_more(layer - 1)

        schedule.run(None)
        launch(C)

    dx_copy.wait()


def backward(y_cot, tables, vectors, places, weights, saved):
    dma, one = pltpu.SemaphoreType.DMA, (1,)
    pair, wide, row = (len(HALVES),), (SEQ, WIDTH), one + (N_VEC,)
    shapes = [(wide, BF16), ((LAYERS, ROWS, PAIR), BF16)]
    shapes += [((LAYERS, groups, ROWS, width), BF16) for groups, width in ((*one, HIDDEN), (SIDE, WIDTH), (*one, QKV), (*one, WIDTH))]
    in_vmem = len(shapes)
    shapes += [((LAYERS, CORES, SEQ, width), BF16) for width in (TILE, SIDE * TILE, PARTS * TILE)]
    blocks = [(CORES, ROWS, width) for wave in WAVES for width in wave]
    shapes += [((LAYERS,) + pair + CHIPS + block, F32) for block in blocks]
    tile = (CORES, ROWS)
    scratch = [(pair + pair + CHIPS[1:] + tile + (WAVES[0][0],), F32), (pair + CHIPS[1:] + tile + (TILE,), F32), (pair + CHIPS + tile + (CORES * WAVES[0][0],), F32), ((SIDE, WIDTH, WIDTH), BF16), ((CORES * SEQ, SIDE * TILE), BF16)]
    scratch += [(pair + shape, BF16) for shape in ((WIDTH, TILE), (TILE, WIDTH))]
    scratch += [(pair + (SEQ, TILE), F32), (wide, F32), (wide, F32), (wide, BF16)] + [(pair + (PAIR, CORES * SEQ), F32)] * CORES
    scratch += [((SEQ, QKV), BF16), (pair + (SEQ, TILE), BF16), ((SEQ, QKV), BF16), (wide, BF16), (wide, BF16), ((LAYERS,) + row, F32),
                ((PARTNERS,) + row, F32)]
    slots = (len(WAVES), AXES) + pair + (LAST + 1,)
    sems = [dma(shape) for shape in ((len(WAVES), AXES, SIDE), slots, (AXES,) + pair, pair, (SIDE, AXES), (AXES, CORES), pair + (PARTS,), (AXES,),
                                     (SIDE,), pair, pair, pair + (N_TILES,), pair + (PARTNERS,))]
    late = [(pair + block[1:], F32) for block in blocks] + [(pair + lead + block, F32) for block in blocks for lead in LEADS]
    outs = pl.pallas_call(
        backward_kernel,
        out_shape=[jax.ShapeDtypeStruct(*s) for s in shapes],
        in_specs=[ANY] + [IN_VMEM] * AXES + [ANY] * (PARTNERS + 1),
        input_output_aliases={SIDE + PARTNERS: in_vmem},
        out_specs=[ANY] + [IN_VMEM] * (in_vmem - 1) + [ANY] * (len(shapes) - in_vmem),
        scratch_shapes=[pltpu.VMEM(*s) for s in scratch] + sems + [pltpu.SemaphoreType.REGULAR((SIDE,))]
        + [pltpu.VMEM(*s) for s in late],
        compiler_params=pltpu.CompilerParams(collective_id=1, has_side_effects=True, vmem_limit_bytes=VMEM_LIMIT),
        name='backward_layers',
    )(y_cot, tables, vectors, places, *weights, *saved)
    d_x, small, *sums = outs[:in_vmem]
    return d_x, small[:, 0], [s.reshape((LAYERS, -1, s.shape[-1])) for s in sums]


def finish_kernel(*refs):
    n_large = CORES + AXES
    large, small_ref, refs = refs[:n_large], refs[n_large], refs[n_large + 1:]
    outs, small_outs, refs = refs[:n_large], refs[n_large:n_large + len(SHARES)], refs[n_large + len(SHARES):]
    held, sems = refs[:n_large], refs[n_large]
    loads = start([pltpu.make_async_copy(src, dst, sems.at[n]) for n, (src, dst) in enumerate(zip(large, held))])
    first = 0
    for share, out in zip(SHARES, small_outs):
        out[...] = small_ref[:, first:first + share]
        first += share
    stores = []
    for load, src, dst in zip(loads, held, outs):
        load.wait()
        stores += start([pltpu.make_async_copy(src, dst, sems.at[n_large + len(stores)])])
    wait(stores)


def finish(large, small):
    shapes = [jax.ShapeDtypeStruct(t.shape, BF16) for t in large] + [jax.ShapeDtypeStruct((LAYERS, share), BF16) for share in SHARES]
    outs = pl.pallas_call(
        finish_kernel,
        out_shape=shapes,
        in_specs=[ANY] * len(large) + [IN_VMEM],
        out_specs=[ANY] * len(large) + [IN_VMEM] * len(SHARES),
        scratch_shapes=[pltpu.VMEM(t.shape, BF16) for t in large] + [pltpu.SemaphoreType.DMA((CORES * len(large),))],
        name='finish',
    )(*large, small)
    return outs[:len(large)], outs[len(large):]


def rope_tables():
    rot_dim, f32 = HEAD // SIDE, np.float32
    inv_freq = f32(1.0) / f32(10000.0) ** (np.arange(0, rot_dim, 2, dtype=f32) / f32(rot_dim))
    angles = np.arange(SEQ, dtype=f32)[:, None] * inv_freq[None, :]
    cos, sin = np.cos(angles), np.sin(angles)
    zero = np.zeros_like(sin)
    rest = np.zeros((SEQ, HEAD - rot_dim), f32)
    tables = ([cos, cos, rest + f32(1.0)], [-sin, zero, rest], [zero, sin, rest])
    return jnp.asarray(np.stack([np.tile(np.concatenate(table, axis=1), (1, 2)) for table in tables]).astype(f32))


def heads_last(tensor):
    lead = tensor.shape[:-2]
    return tensor.reshape(lead + (HEADS, PARTS, HEAD)).swapaxes(-3, -2).reshape(lead + (QKV,))


def heads_first(tensor):
    lead = tensor.shape[:-1]
    return tensor.reshape(lead + (PARTS, HEADS, HEAD)).swapaxes(-3, -2).reshape(lead + (HEADS, PARTS * HEAD))


def vector_places():
    shard, lane, first = [], [], 0
    for k, (share, size) in enumerate(zip(SHARES, SIZES)):
        place = np.arange(size)
        if k == QKV_BIAS:
            place = heads_last(place.reshape(HEADS, -1))
        shard.append(place // share)
        lane.append(first + place % share)
        first += share
    return jnp.asarray(np.stack([np.concatenate(shard), np.concatenate(lane)]).astype(np.int32))


def solution(mesh):
    shard_axes = ('node', 'local')
    act_spec = P(shard_axes)
    param_spec = P(None, shard_axes)

    def device_step(x, y_cot, ln1_gain, ln1_bias, qkv_weight, qkv_bias, out_weight, out_bias,
                    ln2_gain, ln2_bias, up_weight, up_bias, down_weight, down_bias):
        tables, places = rope_tables(), vector_places()
        small = (ln1_gain, ln1_bias, ln2_gain, ln2_bias, qkv_bias, out_bias, up_bias, down_bias)
        small_tile = jnp.pad(jnp.concatenate(small, axis=1), ((0, ROWS - LAYERS), (0, PAIR - sum(SHARES))))
        mix = jnp.concatenate([heads_last(qkv_weight), out_weight], axis=-1)
        *weights, _, vectors, dout_cols, y_out, hidden, n1, n2, ctx, act, qkv, pre = forward(
            x[0], y_cot[0], (up_weight, down_weight, mix), small_tile, tables, places)
        weights = [tensor.reshape((LAYERS, -1, tensor.shape[-1])) for tensor in weights]
        d_x, small_sums, (up, down, qkv, out) = backward(
            y_cot[0], tables, vectors, places, weights, (hidden, n1, n2, ctx, act, qkv, pre, dout_cols))
        (y_out, d_x, up, down, out), (g1, b1, g2, b2, qb, ob, ub, db) = finish((y_out, d_x, up, down, out), small_sums)
        return (y_out[None], d_x[None], g1, b1, heads_first(qkv), qb, out, ob, g2, b2, up, ub, down, db)

    return jax.shard_map(device_step, mesh=mesh,
                         in_specs=(act_spec, act_spec) + (param_spec,) * 12,
                         out_specs=(act_spec, act_spec) + (param_spec,) * 12,
                         check_vma=False)
```

profile of v0, /device:TPU:1, one launch (start us, length us, event | category | flops | bytes accessed | tf_op | source)
XLA Modules:
  0.0 362.2 jit_solution(10664639544437030689)
XLA Ops:
  0.6 0.9 concatenate.7
  1.5 0.6 pad.4.small_ref
  2.1 1.0 reshape.55
  3.2 0.2 reshape.56
  3.3 1.4 pad_maximum_fusion.mix_s
  4.8 131.5 %forward_layers.1 = (bf16[2,4,4,4,2,8,4096]{6,5,4,3,2,1,0:T(8,128)(2,1)}, bf16[2,4,4,4,2,32,1024]{6,5,4,3,2,1,0:T(8,128)(2,1)}, bf16[2,4,4,4,2,8,4096]{6,5,4,3,2...) custom-call(bf16[384,1024]{1,0:T(8,128)(2,1)} %bitcast.29, ...), custom_call_target="tpu_custom_call" | custom-call | tf_op jit(solution)/shard_map/forward_layers/pallas_call | solution.py:539
  136.2 219.0 %backward_layers.1 = (bf16[384,1024]{1,0:T(8,128)(2,1)}, bf16[2,8,128]{2,1,0:T(8,128)(2,1)}, bf16[2,1,8,4096]{3,2,1,0:T(8,128)(2,1)}, bf16[2,4,8,1024]{3,2,1,0:T...) custom-call(bf16[384,1024]{1,0:T(8,128)(2,1)} %bitcast.26, ...), custom_call_target="tpu_custom_call", output_to_operand_aliasing={{6}: (14, {})} | custom-call | tf_op jit(solution)/shard_map/backward_layers/pallas_call | solution.py:1274
  355.3 0.7 copy.35
  356.0 0.5 slice_bitcast_fusion.refs_5_
  356.5 3.6 %finish.1 = (bf16[384,1024]{1,0:T(8,128)(2,1)}, bf16[384,1024]{1,0:T(8,128)(2,1)}, bf16[2,8,4096]{2,1,0:T(8,128)(2,1)}, bf16[2,32,1024]{2,1,0:T(8,128)(2,1)}, bf...) custom-call(bf16[384,1024]{1,0:T(8,128)(2,1)} %get-tuple-element.46., ...), custom_call_target="tpu_custom_call" | custom-call | tf_op jit(solution)/shard_map/finish/pallas_call | solution.py:1308
  360.1 1.1 reshape_reshape.3
  361.2 0.1 copy.38
  361.4 0.9 reshape.63
  (1 shorter events, 0.0 us)
where the time goes:
time: 363 us; the launch traced here: 362 us
  Pallas kernels  354 us (98%)
  local copies, waits for them, and re-layouts  5.92 us (2%)
    pallas_call x1, Pallas kernels, backward(): pl.pallas_call(backward_kernel, out_shape=[jax.ShapeDtypeStruct(*s) for s...  219 us
    pallas_call x1, Pallas kernels, forward(): pl.pallas_call(forward_kernel, out_shape=[jax.ShapeDtypeStruct(*s) for s...  131 us

commit v1 on v0

--- a/solution.py
+++ b/solution.py
@@ -1201,9 +1201,20 @@
                     weight_load(layer, k, k + 1).wait()
                     dn1[...] += dot_t(dqkv_v[:, lanes(k * WIDTH, WIDTH)], big_v[k + 1])
 
-            start(tokens_load(layer, n1_hbm, A, B))
+                    @pl.when(k == A)
+                    def _():
+                        start(tokens_load(layer, n1_hbm, A, B))
 
         schedule.passed(US_NORM)
+
+        @working
+        def _():
+            wait(exchange(layer, B, dqkv_v, dqkv_cols))
+            gradient_loads(C, dqkv_cols)
+            wait(tokens_load(layer, n1_hbm, A, B))
+
+        with jax.named_scope('dw2'):
+            gradient_wave(C, dqkv_cols, B, A, (A, B, C))
 
         @working
         def _():
@@ -1223,13 +1234,6 @@
                     d_h = inverse * (d_scaled - row_mean(d_scaled) - scaled * row_mean(d_scaled * scaled))
                     dh_v[rows, :] = (dh_v[rows, :].astype(F32) + d_h).astype(BF16)
 
-        schedule.passed(US_NORM)
-        @working
-        def _():
-            wait(exchange(layer, B, dqkv_v, dqkv_cols))
-            gradient_loads(C, dqkv_cols)
-            wait(tokens_load(layer, n1_hbm, A, B))
-
         @pl.when(turn_no == A)
         def _():
             start(exchange(layer - 1, A, dh_v, dout_cols))
@@ -1237,15 +1241,13 @@
         @pl.when(turn_no == B)
         def _():
             dx_copy.start()
-
-        with jax.named_scope('dw2'):
-            gradient_wave(C, dqkv_cols, B, A, (A, B, C))
 
         @pl.when(turn_no == A)
         def _():
             prefetch(layer - 1)
             prefetch_more(layer - 1)
 
+        schedule.now += US_NORM
         schedule.run(None)
         launch(C)
 

time: 363 us -> 363 us (level)
  no operation moved by 1% of the time
where the time goes in v1:
time: 363 us; the launch traced here: 362 us
  Pallas kernels  354 us (98%)
  local copies, waits for them, and re-layouts  5.92 us (2%)
    pallas_call x1, Pallas kernels, backward(): pl.pallas_call(backward_kernel, out_shape=[jax.ShapeDtypeStruct(*s) for s...  219 us
    pallas_call x1, Pallas kernels, forward(): pl.pallas_call(forward_kernel, out_shape=[jax.ShapeDtypeStruct(*s) for s...  131 us

profile of v1, /device:TPU:1, one launch (start us, length us, event | category | flops | bytes accessed | tf_op | source)
XLA Modules:
  0.0 362.2 jit_solution(7472457865113782625)
XLA Ops:
  0.6 0.9 concatenate.7
  1.5 0.6 pad.4.small_ref
  2.1 1.0 reshape.55
  3.2 0.2 reshape.56
  3.3 1.4 pad_maximum_fusion.mix_s
  4.8 131.5 %forward_layers.1 = (bf16[2,4,4,4,2,8,4096]{6,5,4,3,2,1,0:T(8,128)(2,1)}, bf16[2,4,4,4,2,32,1024]{6,5,4,3,2,1,0:T(8,128)(2,1)}, bf16[2,4,4,4,2,8,4096]{6,5,4,3,2...) custom-call(bf16[384,1024]{1,0:T(8,128)(2,1)} %bitcast.29, ...), custom_call_target="tpu_custom_call" | custom-call | tf_op jit(solution)/shard_map/forward_layers/pallas_call | solution.py:539
  136.2 219.0 %backward_layers.1 = (bf16[384,1024]{1,0:T(8,128)(2,1)}, bf16[2,8,128]{2,1,0:T(8,128)(2,1)}, bf16[2,1,8,4096]{3,2,1,0:T(8,128)(2,1)}, bf16[2,4,8,1024]{3,2,1,0:T...) custom-call(bf16[384,1024]{1,0:T(8,128)(2,1)} %bitcast.26, ...), custom_call_target="tpu_custom_call", output_to_operand_aliasing={{6}: (14, {})} | custom-call | tf_op jit(solution)/shard_map/backward_layers/pallas_call | solution.py:1276
  355.3 0.7 copy.35
  355.9 0.5 slice_bitcast_fusion.refs_5_
  356.5 3.6 %finish.1 = (bf16[384,1024]{1,0:T(8,128)(2,1)}, bf16[384,1024]{1,0:T(8,128)(2,1)}, bf16[2,8,4096]{2,1,0:T(8,128)(2,1)}, bf16[2,32,1024]{2,1,0:T(8,128)(2,1)}, bf...) custom-call(bf16[384,1024]{1,0:T(8,128)(2,1)} %get-tuple-element.46., ...), custom_call_target="tpu_custom_call" | custom-call | tf_op jit(solution)/shard_map/finish/pallas_call | solution.py:1310
  360.1 1.1 reshape_reshape.3
  361.2 0.1 copy.38
  361.3 0.9 reshape.63
  (1 shorter events, 0.0 us)

commit v2 on v1

--- a/solution.py
+++ b/solution.py
@@ -553,7 +553,7 @@
 STEPS = ((1, (2,)), (0, ()), (2, (4, 3)), (4, (5,)), (3, ()), (5, (6, 7, 8)), (8, (9,)), (9, ()))
 LAST = AXES * AXES
 CARRIED = ((0, 6, 0), (1, 4, 0), (2, 0, 0))
-US_COLUMN, US_HOP, US_ADD, US_STEP = 0.022, 2.5, 0.0013, 0.2
+US_COLUMN, US_HOP, US_ADD, US_STEP = 0.021, 2.5, 0.0013, 0.2
 US_FIRST, US_OUT, US_TILE, US_GRADIENT, US_PAIR, US_NORM = 2, 1.4, 1.6, 0.0035, 3.6, 2.7
 
 

time: 363 us -> 363 us (level)
  no operation moved by 1% of the time
where the time goes in v2:
time: 363 us; the launch traced here: 362 us
  Pallas kernels  354 us (98%)
  local copies, waits for them, and re-layouts  5.92 us (2%)
    pallas_call x1, Pallas kernels, backward(): pl.pallas_call(backward_kernel, out_shape=[jax.ShapeDtypeStruct(*s) for s...  219 us
    pallas_call x1, Pallas kernels, forward(): pl.pallas_call(forward_kernel, out_shape=[jax.ShapeDtypeStruct(*s) for s...  131 us

profile of v2, /device:TPU:1, one launch (start us, length us, event | category | flops | bytes accessed | tf_op | source)
XLA Modules:
  0.0 362.3 jit_solution(17897148700168726207)
XLA Ops:
  0.6 0.9 concatenate.7
  1.5 0.6 pad.4.small_ref
  2.1 1.0 reshape.55
  3.2 0.2 reshape.56
  3.3 1.4 pad_maximum_fusion.mix_s
  4.8 131.5 %forward_layers.1 = (bf16[2,4,4,4,2,8,4096]{6,5,4,3,2,1,0:T(8,128)(2,1)}, bf16[2,4,4,4,2,32,1024]{6,5,4,3,2,1,0:T(8,128)(2,1)}, bf16[2,4,4,4,2,8,4096]{6,5,4,3,2...) custom-call(bf16[384,1024]{1,0:T(8,128)(2,1)} %bitcast.29, ...), custom_call_target="tpu_custom_call" | custom-call | tf_op jit(solution)/shard_map/forward_layers/pallas_call | solution.py:539
  136.2 219.1 %backward_layers.1 = (bf16[384,1024]{1,0:T(8,128)(2,1)}, bf16[2,8,128]{2,1,0:T(8,128)(2,1)}, bf16[2,1,8,4096]{3,2,1,0:T(8,128)(2,1)}, bf16[2,4,8,1024]{3,2,1,0:T...) custom-call(bf16[384,1024]{1,0:T(8,128)(2,1)} %bitcast.26, ...), custom_call_target="tpu_custom_call", output_to_operand_aliasing={{6}: (14, {})} | custom-call | tf_op jit(solution)/shard_map/backward_layers/pallas_call | solution.py:1276
  355.3 0.7 copy.35
  356.0 0.5 slice_bitcast_fusion.refs_5_
  356.5 3.6 %finish.1 = (bf16[384,1024]{1,0:T(8,128)(2,1)}, bf16[384,1024]{1,0:T(8,128)(2,1)}, bf16[2,8,4096]{2,1,0:T(8,128)(2,1)}, bf16[2,32,1024]{2,1,0:T(8,128)(2,1)}, bf...) custom-call(bf16[384,1024]{1,0:T(8,128)(2,1)} %get-tuple-element.46., ...), custom_call_target="tpu_custom_call" | custom-call | tf_op jit(solution)/shard_map/finish/pallas_call | solution.py:1310
  360.2 1.1 reshape_reshape.3
  361.3 0.1 copy.38
  361.4 0.9 reshape.63
  (1 shorter events, 0.0 us)
